TPU v7x, 32 devices: a whole 2x2x4 slice. The times are simulated.
32 devices in a mesh: rows: 4 (over y, x), cols: 8 (over z, core).
Axes of the slice: x: 2, y: 2, z: 4, core: 2. Of those that a mesh axis runs over, the one named last changes fastest.
Arguments:
- latent1: bfloat16 [64, 512, 320], P('rows', 'cols'), may hold values from -15 to 15, as said below
- norm1a_g: float32 [320], replicated, may hold values from 0.25 to 1.75
- norm1a_b: float32 [320], replicated, may hold values from -3 to 3
- conv1a_w: bfloat16 [3, 3, 320, 320], replicated, may hold values from -0.109375 to 0.109375
- norm1b_g: float32 [320], replicated, may hold values from 0.25 to 1.75
- norm1b_b: float32 [320], replicated, may hold values from -3 to 3
- conv1b_w: bfloat16 [3, 3, 320, 320], replicated, may hold values from -0.109375 to 0.109375
- conv1b_b: float32 [320], replicated, may hold values from -3 to 3
- feat3: bfloat16 [16, 128, 1280], P('rows', 'cols'), may hold values from -15 to 15, as said below
- adapter3: bfloat16 [16, 128, 1280], P('rows', 'cols'), may hold values from -15 to 15, as said below
- norm3a_g: float32 [1280], replicated, may hold values from 0.25 to 1.75
- norm3a_b: float32 [1280], replicated, may hold values from -3 to 3
- conv3a_w: bfloat16 [3, 3, 1280, 1280], P(None, None, None, 'cols'), may hold values from -0.0546875 to 0.0546875
- norm3b_g: float32 [1280], P('cols'), may hold values from 0.25 to 1.75
- norm3b_b: float32 [1280], P('cols'), may hold values from -3 to 3
- conv3b_w: bfloat16 [3, 3, 1280, 1280], P(None, None, None, 'cols'), may hold values from -0.0546875 to 0.0546875
- conv3b_b: float32 [1280], P('cols'), may hold values from -3 to 3
Outputs:
- out1: bfloat16 [64, 512, 320], P('rows', 'cols')
- out3: bfloat16 [16, 128, 1280], P('rows', None, 'cols')
Inputs may be any that keep to these rules, and one draw needn't show every extreme that they name: `latent1`: real values. `feat3`: real values. `adapter3`: real values.
All inputs are finite; a program needn't handle non-finite values.
Results may differ from a plain program's by a relative error of at most 0.0052.
Values may be sent and summed in bfloat16 or wider, within the bound.
No kernel may reach another device: no remote copies, remote signals or barrier semaphores. Data moves between devices by JAX's collectives and lax.ppermute only.
A program may use at most 128 MiB of HBM per device.

v0:
```python
import jax
import jax.numpy as jnp
from jax import lax
from jax.sharding import PartitionSpec as P

C1 = 320
C3 = 1280
norm_eps = 1e-05


def extended(block, sides, width):
    for axis, dim in sides:
        count = lax.axis_size(axis)
        forward = [(i, i + 1) for i in range(count - 1)]
        backward = [(target, source) for source, target in forward]
        low = lax.ppermute(
            lax.slice_in_dim(block, block.shape[dim] - width, None, axis=dim), axis, forward
        )
        high = lax.ppermute(lax.slice_in_dim(block, 0, width, axis=dim), axis, backward)
        block = jnp.concatenate([low, block, high], axis=dim)
    return block


def conv_valid(padded, kernel):
    return lax.conv_general_dilated(
        padded[None],
        kernel,
        (1, 1),
        "VALID",
        dimension_numbers=("NHWC", "HWIO", "NHWC"),
        preferred_element_type=jnp.float32,
    )[0]


def moments(value, group_width):
    height, width, chans = value.shape
    grouped = value.astype(jnp.float32).reshape(height, width, chans // group_width, group_width)
    return (jnp.sum(grouped, axis=(0, 1, 3)), jnp.sum(grouped * grouped, axis=(0, 1, 3)))


def normalize(value, sums, squares, count, gain, shift):
    height, width, chans = value.shape
    groups = sums.shape[0]
    mean = sums / count
    inverse = lax.rsqrt(squares / count - mean * mean + norm_eps)
    grouped = value.astype(jnp.float32).reshape(height, width, groups, chans // groups)
    normed = ((grouped - mean[:, None]) * inverse[:, None]).reshape(height, width, chans)
    return jax.nn.silu(normed * gain + shift).astype(jnp.bfloat16)


def level3_totals(values, group_width):
    sums, squares = moments(values, group_width)
    return lax.psum((sums, squares), "rows")


def folder(kernel, total, piece):
    height = total.shape[0]
    width = total.shape[1]
    count = piece.shape[2]
    wide = jnp.pad(piece, ((0, 0), (1, 1), (0, 0)))
    taps = [wide[dy : dy + height, dx : dx + width, :] for dy in range(3) for dx in range(3)]
    patches = jnp.concatenate(taps, axis=2).reshape(height * width, 9 * count)
    weights = kernel.reshape(9 * count, kernel.shape[3])
    product = jnp.dot(patches, weights, preferred_element_type=jnp.float32)
    return product.reshape(height, width, kernel.shape[3])


def body(
    latent1,
    norm1a_g,
    norm1a_b,
    conv1a_w,
    norm1b_g,
    norm1b_b,
    conv1b_w,
    conv1b_b,
    feat3,
    adapter3,
    norm3a_g,
    norm3a_b,
    conv3a_w,
    norm3b_g,
    norm3b_b,
    conv3b_w,
    conv3b_b,
):
    rows_one = latent1.shape[0]
    cols_one = latent1.shape[1]
    width_one = C1 // 32
    count_one = rows_one * cols_one * lax.axis_size("rows") * lax.axis_size("cols") * width_one
    sums, squares = moments(latent1, width_one)
    sums, squares = lax.psum((sums, squares), ("rows", "cols"))
    act1 = normalize(latent1, sums, squares, count_one, norm1a_g, norm1a_b)
    padded = extended(act1, (("rows", 0), ("cols", 1)), 1)
    hid1 = conv_valid(padded, conv1a_w)
    sums_two, squares_two = moments(hid1, width_one)
    sums_two, squares_two = lax.psum((sums_two, squares_two), ("rows", "cols"))
    act2 = normalize(hid1, sums_two, squares_two, count_one, norm1b_g, norm1b_b)
    padded_two = extended(act2, (("rows", 0), ("cols", 1)), 1)
    out1 = (latent1.astype(jnp.float32) + conv_valid(padded_two, conv1b_w) + conv1b_b).astype(
        jnp.bfloat16
    )
    joined = (feat3.astype(jnp.float32) + adapter3.astype(jnp.float32)).astype(jnp.bfloat16)
    shard = conv3a_w.shape[3]
    height = feat3.shape[0]
    width = feat3.shape[1] * lax.axis_size("cols")
    width_three = C3 // 32
    count_three = height * width * lax.axis_size("rows") * width_three
    empty = jnp.zeros((height, width, shard), jnp.float32)
    edged_tile = extended(joined, (("rows", 0),), 1)
    whole = lax.all_gather(edged_tile, "cols", axis=1, tiled=True)
    local = lax.dynamic_slice_in_dim(whole[1:-1], lax.axis_index("cols") * shard, shard, 2)
    sums_three, squares_three = level3_totals(whole[1:-1], width_three)
    line_ids = lax.axis_index("rows") * height - 1 + jnp.arange(height + 2, dtype=jnp.int32)
    line_ok = (line_ids >= 0) & (line_ids < height * lax.axis_size("rows"))
    act_whole = normalize(whole, sums_three, squares_three, count_three, norm3a_g, norm3a_b)
    act_whole = jnp.where(line_ok[:, None, None], act_whole, jnp.zeros((), jnp.bfloat16))
    hid3 = conv_valid(jnp.pad(act_whole, ((0, 0), (1, 1), (0, 0))), conv3a_w)
    sums_four, squares_four = moments(hid3, width_three)
    sums_four, squares_four = lax.psum((sums_four, squares_four), "rows")
    act4 = normalize(hid3, sums_four, squares_four, count_three, norm3b_g, norm3b_b)
    edged_two = extended(act4, (("rows", 0),), 1)
    second = folder(conv3b_w, empty, lax.all_gather(edged_two, "cols", axis=2, tiled=True))
    out3 = (local.astype(jnp.float32) + second + conv3b_b).astype(jnp.bfloat16)
    return (out1, out3)


def solution(mesh):
    placed = (
        P("rows", "cols", None),
        P(),
        P(),
        P(),
        P(),
        P(),
        P(),
        P(),
        P("rows", "cols", None),
        P("rows", "cols", None),
        P(),
        P(),
        P(None, None, None, "cols"),
        P("cols"),
        P("cols"),
        P(None, None, None, "cols"),
        P("cols"),
    )
    return jax.shard_map(
        body,
        mesh=mesh,
        in_specs=placed,
        out_specs=(P("rows", "cols", None), P("rows", None, "cols")),
        check_vma=False,
    )
```

profile of v0, /device:TPU:3, one launch (start us, length us, event | category | flops | bytes accessed | tf_op | source)
XLA Modules:
  0.0 271.7 jit_solution(1989159942951387046)
XLA Ops:
  7.2 1.2 add_convert_fusion
  8.4 3.1 %collective-permute-start.8 = (bf16[1,16,1280]{2,1,0:T(8,128)(2,1)S(1)}, bf16[1,16,1280]{2,1,0:T(8,128)(2,1)S(1)}, u32[]{:S(2)}, u32[]{:S(2)}) collective-permute-start(bf16[1,16,1280]{2,1,0:T(8,128)(2,1)S(1)} %get-tuple-element.38), channel_id=1, source_target_pairs={{0,8},{8,16},{16,24},{1,9},{9,17},{17,25},{2,10},{10,18},{18,26},{... | collective-permute-start | bytes 122888 | tf_op jit(solution)/shard_map/ppermute | solution.py:16
  11.6 2.2 collective-permute-start.9
  13.7 3.5 %collective-permute-done.9 = bf16[1,16,1280]{2,1,0:T(8,128)(2,1)S(1)} collective-permute-done((bf16[1,16,1280]{2,1,0:T(8,128)(2,1)S(1)}, bf16[1,16,1280]{2,1,0:T(8,128)(2,1)S(1)}, u32[]{:S(2)}, u32[]{:S(2)}) %collective-permute-start.9) | collective-permute-done | bytes 40992 | tf_op jit(solution)/shard_map/ppermute | solution.py:19
  18.0 1.6 convert_reduce_fusion.1
  21.2 27.1 %all-gather.3.cloned.1.call-done = bf16[6,128,1280]{2,1,0:T(8,128)(2,1)} async-done(((bf16[6,16,1280]{2,1,0:T(8,128)(2,1)}), bf16[6,128,1280]{2,1,0:T(8,128)(2,1)}) %all-gather.3.cloned.1.call-update) | async-done | bytes 1966096 | tf_op jit(solution)/shard_map/all_gather | solution.py:111
  48.3 1.3 slice-done
  49.6 1.4 copy.113
  51.0 1.8 convert_reduce_fusion
  53.2 6.0 %all-reduce.5 = (f32[32]{0:T(128)S(1)}, f32[32]{0:T(128)S(1)}) all-reduce(f32[32]{0:T(128)S(1)} %reduce_sum.145, f32[32]{0:T(128)S(1)} %reduce_sum.115), channel_id=1, replica_groups=mesh['rows'=4,'cols'=8] {'rows'}, use_global_device_ids=true, to_apply=%region_17.18 | all-reduce | flops 64 | bytes 512 | tf_op jit(solution)/shard_map/psum | solution.py:53
  59.5 3.0 %fusion.11 = bf16[6,128,1280]{2,1,0:T(8,128)(2,1)S(1)} fusion(bf16[6,128,1280]{2,1,0:T(8,128)(2,1)} %all-gather.3.cloned.1.call-done, f32[1280]{0:T(1024)S(1)} %copy-done.4, f32[1280]{0:T(1024)S(1)} %copy-done.5, f32[1280]{0:T(1024)S(1)} %mul.156, f32[1280]{0:T(1024)S(1)} %sub.79, pred[6]{0:T(512)(128)(4,1)S(1)} %compare_and_fusion), kind=kLoop, calls=%fused_computation.20 | loop fusion | flops 10813440 | bytes 3952646 | tf_op jit(solution)/shard_map/jit(_where)/select_n | solution.py:117
  63.0 1.5 pad.13
  64.5 4.2 %reshape.81 = bf16[6,1,8,17,1280]{4,3,2,0,1:T(8,128)(2,1)} reshape(bf16[6,1,136,1280]{3,2,0,1:T(8,128)(2,1)} %pad.13) | data formatting | bytes 4177920 | tf_op jit(solution)/shard_map/conv_general_dilated | solution.py:25
  68.7 2.4 copy.104
  71.6 3.5 %select_reduce_fusion.3 = (f32[160]{0:T(256)S(1)}, f32[160]{0:T(256)S(1)}, f32[4,8,17,160]{3,1,2,0:T(8,128)S(1)}) fusion(pred[8,17]{0,1:T(8,128)(4,1)S(1)} %copy-done.18, bf16[3,3,1280,160]{2,3,1,0:T(8,128)(2,1)S(1)} %copy-done.15, bf16[6,1,7,2,1280]{4,2,3,0,1:T(8,128)(2,1)S(1)} %slice.109, bf16[6,1,8,17,1280]{4,2,3,0,1:T(8,128)(2,1)S(1)} %copy.104), kind=kOutput, calls=%fused_computation.73 | convolution fusion | flops 2012927744 | bytes 6339976 | tf_op jit(solution)/shard_map/conv_general_dilated | solution.py:25
  75.5 42.0 %all-reduce.3 = (f32[32]{0:T(128)}, f32[32]{0:T(128)}) all-reduce(f32[32]{0:T(128)S(1)} %copy-done.11, f32[32]{0:T(128)S(1)} %copy-done.12), channel_id=1, replica_groups=mesh['rows'=4,'cols'=8] {'rows','cols'}, use_global_device_ids=true, to_apply=%region_5.6 | all-reduce | flops 64 | bytes 512 | tf_op jit(solution)/shard_map/psum | solution.py:92
  117.5 6.0 %all-reduce.4 = (f32[4]{0:T(128)S(1)}, f32[4]{0:T(128)S(1)}) all-reduce(f32[4]{0:T(128)S(1)} %reduce_sum.151, f32[4]{0:T(128)S(1)} %reduce_sum.148), channel_id=1, replica_groups=mesh['rows'=4,'cols'=8] {'rows'}, use_global_device_ids=true, to_apply=%region_23.24 | all-reduce | flops 8 | bytes 64 | tf_op jit(solution)/shard_map/psum | solution.py:120
  125.3 0.9 copy.114
  126.3 1.2 multiply_convert_fusion.2
  127.5 4.0 %collective-permute-start.10 = (bf16[1,128,160]{1,2,0:T(8,128)(2,1)S(1)}, bf16[1,128,160]{1,2,0:T(8,128)(2,1)S(1)}, u32[]{:S(2)}, u32[]{:S(2)}) collective-permute-start(bf16[1,128,160]{1,2,0:T(8,128)(2,1)S(1)} %get-tuple-element.36), channel_id=1, source_target_pairs={{0,8},{8,16},{16,24},{1,9},{9,17},{17,25},{2,10},{10,18},{18,26},{... | collective-permute-start | bytes 122888 | tf_op jit(solution)/shard_map/ppermute | solution.py:16
  131.5 1.9 collective-permute-start.11
  133.8 3.3 %collective-permute-done.11 = bf16[1,128,160]{1,2,0:T(8,128)(2,1)S(1)} collective-permute-done((bf16[1,128,160]{1,2,0:T(8,128)(2,1)S(1)}, bf16[1,128,160]{1,2,0:T(8,128)(2,1)S(1)}, u32[]{:S(2)}, u32[]{:S(2)}) %collective-permute-start.11) | collective-permute-done | bytes 40992 | tf_op jit(solution)/shard_map/ppermute | solution.py:19
  137.1 0.7 pad_maximum_fusion.1
  137.9 0.8 fusion.20
  138.8 1.9 collective-permute-start
  140.8 3.4 %collective-permute-start.1 = (bf16[1,64,320]{2,0,1:T(2,128)(2,1)S(1)}, bf16[1,64,320]{2,0,1:T(2,128)(2,1)S(1)}, u32[]{:S(2)}, u32[]{:S(2)}) collective-permute-start(bf16[1,64,320]{2,0,1:T(2,128)(2,1)S(1)} %get-tuple-element.35), channel_id=1, source_target_pairs={{8,0},{16,8},{24,16},{9,1},{17,9},{25,17},{10,2},{18,10},{26,18},{... | collective-permute-start | bytes 122888 | tf_op jit(solution)/shard_map/ppermute | solution.py:19
  144.2 2.8 %collective-permute-done.1 = bf16[1,64,320]{2,0,1:T(2,128)(2,1)S(1)} collective-permute-done((bf16[1,64,320]{2,0,1:T(2,128)(2,1)S(1)}, bf16[1,64,320]{2,0,1:T(2,128)(2,1)S(1)}, u32[]{:S(2)}, u32[]{:S(2)}) %collective-permute-start.1) | collective-permute-done | bytes 40992 | tf_op jit(solution)/shard_map/ppermute | solution.py:19
  147.0 9.3 %collective-permute-start.2 = (bf16[18,1,320]{2,0,1:T(8,128)(2,1)S(1)}, bf16[18,1,320]{2,0,1:T(8,128)(2,1)S(1)}, u32[]{:S(2)}, u32[]{:S(2)}) collective-permute-start(bf16[18,1,320]{2,0,1:T(8,128)(2,1)S(1)} %get-tuple-element.30), channel_id=1, source_target_pairs={{0,1},{1,2},{2,3},{3,4},{4,5},{5,6},{6,7},{8,9},{9,10},{10,11},{11... | collective-permute-start | bytes 34568 | tf_op jit(solution)/shard_map/ppermute | solution.py:16
  156.3 2.1 collective-permute-start.3
  158.4 4.4 %collective-permute-done.3 = bf16[18,1,320]{2,0,1:T(8,128)(2,1)S(1)} collective-permute-done((bf16[18,1,320]{2,0,1:T(8,128)(2,1)S(1)}, bf16[18,1,320]{2,0,1:T(8,128)(2,1)S(1)}, u32[]{:S(2)}, u32[]{:S(2)}) %collective-permute-start.3) | collective-permute-done | bytes 11552 | tf_op jit(solution)/shard_map/ppermute | solution.py:19
  162.8 0.7 maximum_bitcast_fusion
  164.2 5.1 %select_reduce_fusion.1 = (f32[320]{0:T(512)S(1)}, f32[320]{0:T(512)S(1)}, f32[16,8,9,320]{3,1,2,0:T(8,128)}) fusion(pred[8,9]{0,1:T(8,128)(4,1)S(1)} %copy-done.19, bf16[3,3,320,320]{3,2,1,0:T(8,128)(2,1)S(1)} %copy-done, bf16[18,1,7,2,320]{4,2,3,0,1:T(8,128)(2,1)S(1)} %slice.100, bf16[18,1,8,9,320]{4,2,3,0,1:T(8,128)(2,1)S(1)} %copy.97), kind=kOutput, calls=%fused_computation.22 | convolution fusion | flops 2128619008 | bytes 4311112 | tf_op jit(solution)/shard_map/conv_general_dilated | solution.py:25
  169.8 37.3 %all-reduce.2 = (f32[32]{0:T(128)S(1)}, f32[32]{0:T(128)S(1)}) all-reduce(f32[32]{0:T(128)S(1)} %reduce_sum.112, f32[32]{0:T(128)S(1)} %reduce_sum.106), channel_id=1, replica_groups=mesh['rows'=4,'cols'=8] {'rows','cols'}, use_global_device_ids=true, to_apply=%region_11.12 | all-reduce | flops 64 | bytes 512 | tf_op jit(solution)/shard_map/psum | solution.py:97
  207.5 1.8 copy.98
  210.0 3.1 %collective-permute-start.4 = (bf16[1,64,320]{2,0,1:T(2,128)(2,1)S(1)}, bf16[1,64,320]{2,0,1:T(2,128)(2,1)S(1)}, u32[]{:S(2)}, u32[]{:S(2)}) collective-permute-start(bf16[1,64,320]{2,0,1:T(2,128)(2,1)S(1)} %get-tuple-element.32), channel_id=1, source_target_pairs={{0,8},{8,16},{16,24},{1,9},{9,17},{17,25},{2,10},{10,18},{18,26},{... | collective-permute-start | bytes 122888 | tf_op jit(solution)/shard_map/ppermute | solution.py:16
  213.1 2.2 collective-permute-start.5
  215.4 4.0 %collective-permute-done.5 = bf16[1,64,320]{2,0,1:T(2,128)(2,1)S(1)} collective-permute-done((bf16[1,64,320]{2,0,1:T(2,128)(2,1)S(1)}, bf16[1,64,320]{2,0,1:T(2,128)(2,1)S(1)}, u32[]{:S(2)}, u32[]{:S(2)}) %collective-permute-start.5) | collective-permute-done | bytes 40992 | tf_op jit(solution)/shard_map/ppermute | solution.py:19
  219.4 6.1 %collective-permute-start.6 = (bf16[18,1,320]{2,0,1:T(8,128)(2,1)S(1)}, bf16[18,1,320]{2,0,1:T(8,128)(2,1)S(1)}, u32[]{:S(2)}, u32[]{:S(2)}) collective-permute-start(bf16[18,1,320]{2,0,1:T(8,128)(2,1)S(1)} %get-tuple-element.28), channel_id=1, source_target_pairs={{0,1},{1,2},{2,3},{3,4},{4,5},{5,6},{6,7},{8,9},{9,10},{10,11},{11... | collective-permute-start | bytes 34568 | tf_op jit(solution)/shard_map/ppermute | solution.py:16
  225.5 1.9 collective-permute-start.7
  227.5 7.4 %copy.111 = bf16[3,3,1280,160]{2,1,0,3:T(4,128)(2,1)} copy(bf16[3,3,1280,160]{2,3,1,0:T(8,128)(2,1)} %param.32) | data formatting | bytes 7372800 | tf_op args[15]
  234.9 9.4 %reshape.109 = bf16[11520,160,1]{0,1,2:T(8,128)(2,1)} reshape(bf16[3,3,1280,160]{2,1,0,3:T(4,128)(2,1)} %copy.111) | data formatting | bytes 7372800 | tf_op jit(solution)/shard_map/reshape | solution.py:63
  244.3 0.7 maximum_bitcast_fusion.1
  245.4 1.2 copy-done.16
  246.6 3.8 %convolution_select_fusion = f32[16,8,9,320]{3,1,2,0:T(8,128)S(1)} fusion(bf16[3,3,320,320]{3,2,1,0:T(8,128)(2,1)S(1)} %copy-done.16, bf16[18,1,7,2,320]{4,2,3,0,1:T(8,128)(2,1)S(1)} %slice.104, bf16[18,1,8,9,320]{4,2,3,0,1:T(8,128)(2,1)S(1)} %copy.100, pred[8,9]{0,1:T(8,128)(4,1)S(1)} %copy-done.19), kind=kOutput, calls=%fused_computation.42 | convolution fusion | flops 2126776320 | bytes 4308552 | tf_op jit(solution)/shard_map/conv_general_dilated | solution.py:25
  251.7 1.1 copy.112
  252.8 2.7 copy.107
  257.6 1.6 copy-done.3
  259.2 5.7 %fusion.45 = bf16[4,128,160]{1,2,0:T(8,128)(2,1)} fusion(bf16[4,128,11520]{2,1,0:T(8,128)(2,1)S(1)} %slice_dynamic-update-slice_fusion.3, bf16[11520,160,1]{0,1,2:T(8,128)(2,1)S(1)} %copy-done.3, f32[160]{0:T(256)S(1)} %copy-done.17, bf16[4,128,1280]{1,2,0:T(8,128)(2,1)} %copy.113, s32[]{:T(128)S(6)} %select_n.7), kind=kOutput, calls=%fused_computation.69 | convolution fusion | flops 1887764480 | bytes 15811204 | tf_op jit(solution)/shard_map/dot_general | solution.py:64
  (117 shorter events, 12.8 us)
Async XLA Ops:
  7.2 156.8 %copy-start = (bf16[3,3,320,320]{3,2,1,0:T(8,128)(2,1)S(1)}, bf16[3,3,320,320]{3,2,1,0:T(8,128)(2,1)}, u32[]{:S(2)}) copy-start(bf16[3,3,320,320]{3,2,1,0:T(8,128)(2,1)} %param.20) | copy-start | bytes 5529604
  7.2 41.1 %all-gather.3.cloned.1.call-start = ((), (), s32[]{:S(2)}) async-start(), calls=%async_computation | async-start | bytes 2211840 | tf_op jit(solution)/shard_map/all_gather | solution.py:111
  8.4 5.3 %collective-permute-start.8 = (bf16[1,16,1280]{2,1,0:T(8,128)(2,1)S(1)}, bf16[1,16,1280]{2,1,0:T(8,128)(2,1)S(1)}, u32[]{:S(2)}, u32[]{:S(2)}) collective-permute-start(bf16[1,16,1280]{2,1,0:T(8,128)(2,1)S(1)} %get-tuple-element.38), channel_id=1, source_target_pairs={{0,8},{8,16},{16,24},{1,9},{9,17},{17,25},{2,10},{10,18},{18,26},{... | collective-permute-start | bytes 122888 | tf_op jit(solution)/shard_map/ppermute | solution.py:16
  11.6 5.6 %collective-permute-start.9 = (bf16[1,16,1280]{2,1,0:T(8,128)(2,1)S(1)}, bf16[1,16,1280]{2,1,0:T(8,128)(2,1)S(1)}, u32[]{:S(2)}, u32[]{:S(2)}) collective-permute-start(bf16[1,16,1280]{2,1,0:T(8,128)(2,1)S(1)} %get-tuple-element.39), channel_id=1, source_target_pairs={{8,0},{16,8},{24,16},{9,1},{17,9},{25,17},{10,2},{18,10},{26,18},{... | collective-permute-start | bytes 122888 | tf_op jit(solution)/shard_map/ppermute | solution.py:19
  17.9 234.8 %all-gather.5.cloned.1.call-start = ((), (), s32[]{:S(2)}) async-start(), calls=%async_computation.1 | async-start | bytes 2211840 | tf_op jit(solution)/shard_map/all_gather | solution.py:123
  48.3 1.3 slice-start
  49.6 9.9 %copy-start.4 = (f32[1280]{0:T(1024)S(1)}, f32[1280]{0:T(1024)}, u32[]{:S(2)}) copy-start(f32[1280]{0:T(1024)} %param.28) | copy-start | bytes 15364
  49.6 10.0 %copy-start.5 = (f32[1280]{0:T(1024)S(1)}, f32[1280]{0:T(1024)}, u32[]{:S(2)}) copy-start(f32[1280]{0:T(1024)} %param.27) | copy-start | bytes 15364
  68.7 2.9 %copy-start.15 = (bf16[3,3,1280,160]{2,3,1,0:T(8,128)(2,1)S(1)}, bf16[3,3,1280,160]{2,3,1,0:T(8,128)(2,1)}, u32[]{:S(2)}) copy-start(bf16[3,3,1280,160]{2,3,1,0:T(8,128)(2,1)} %param.29) | copy-start | bytes 11059204
  68.7 2.9 %copy-start.18 = (pred[8,17]{0,1:T(8,128)(4,1)S(1)}, pred[8,17]{0,1:T(8,128)(4,1)}, u32[]{:S(2)}) copy-start(pred[8,17]{0,1:T(8,128)(4,1)} %constant.75) | copy-start | bytes 412
  71.6 3.9 %copy-start.11 = (f32[32]{0:T(128)S(1)}, f32[32]{0:T(128)}, u32[]{:S(2)}) copy-start(f32[32]{0:T(128)} %reduce_sum.100) | copy-start | bytes 388
  71.6 3.9 %copy-start.12 = (f32[32]{0:T(128)S(1)}, f32[32]{0:T(128)}, u32[]{:S(2)}) copy-start(f32[32]{0:T(128)} %reduce_sum.97) | copy-start | bytes 388
  125.0 12.9 %copy-start.2 = (bf16[16,64,320]{2,1,0:T(8,128)(2,1)S(1)}, bf16[16,64,320]{2,1,0:T(8,128)(2,1)}, u32[]{:S(2)}) copy-start(bf16[16,64,320]{2,1,0:T(8,128)(2,1)} %param.17) | copy-start | bytes 1966084
  125.2 8.2 %copy-start.13 = (f32[32]{0:T(128)S(1)}, f32[32]{0:T(128)}, u32[]{:S(2)}) copy-start(f32[32]{0:T(128)} %get-tuple-element.22) | copy-start | bytes 388
  125.2 8.2 %copy-start.14 = (f32[32]{0:T(128)S(1)}, f32[32]{0:T(128)}, u32[]{:S(2)}) copy-start(f32[32]{0:T(128)} %get-tuple-element.23) | copy-start | bytes 388
  125.3 12.6 %copy-start.6 = (f32[320]{0:T(512)S(1)}, f32[320]{0:T(512)}, u32[]{:S(2)}) copy-start(f32[320]{0:T(512)} %param.19) | copy-start | bytes 3844
  125.3 12.6 %copy-start.7 = (f32[320]{0:T(512)S(1)}, f32[320]{0:T(512)}, u32[]{:S(2)}) copy-start(f32[320]{0:T(512)} %param.18) | copy-start | bytes 3844
  127.5 6.3 %collective-permute-start.10 = (bf16[1,128,160]{1,2,0:T(8,128)(2,1)S(1)}, bf16[1,128,160]{1,2,0:T(8,128)(2,1)S(1)}, u32[]{:S(2)}, u32[]{:S(2)}) collective-permute-start(bf16[1,128,160]{1,2,0:T(8,128)(2,1)S(1)} %get-tuple-element.36), channel_id=1, source_target_pairs={{0,8},{8,16},{16,24},{1,9},{9,17},{17,25},{2,10},{10,18},{18,26},{... | collective-permute-start | bytes 122888 | tf_op jit(solution)/shard_map/ppermute | solution.py:16
  131.5 5.6 %collective-permute-start.11 = (bf16[1,128,160]{1,2,0:T(8,128)(2,1)S(1)}, bf16[1,128,160]{1,2,0:T(8,128)(2,1)S(1)}, u32[]{:S(2)}, u32[]{:S(2)}) collective-permute-start(bf16[1,128,160]{1,2,0:T(8,128)(2,1)S(1)} %get-tuple-element.37), channel_id=1, source_target_pairs={{8,0},{16,8},{24,16},{9,1},{17,9},{25,17},{10,2},{18,10},{26,18},{... | collective-permute-start | bytes 122888 | tf_op jit(solution)/shard_map/ppermute | solution.py:19
  138.8 5.4 %collective-permute-start = (bf16[1,64,320]{2,0,1:T(2,128)(2,1)S(1)}, bf16[1,64,320]{2,0,1:T(2,128)(2,1)S(1)}, u32[]{:S(2)}, u32[]{:S(2)}) collective-permute-start(bf16[1,64,320]{2,0,1:T(2,128)(2,1)S(1)} %get-tuple-element.34), channel_id=1, source_target_pairs={{0,8},{8,16},{16,24},{1,9},{9,17},{17,25},{2,10},{10,18},{18,26},{... | collective-permute-start | bytes 122888 | tf_op jit(solution)/shard_map/ppermute | solution.py:16
  140.8 6.3 %collective-permute-start.1 = (bf16[1,64,320]{2,0,1:T(2,128)(2,1)S(1)}, bf16[1,64,320]{2,0,1:T(2,128)(2,1)S(1)}, u32[]{:S(2)}, u32[]{:S(2)}) collective-permute-start(bf16[1,64,320]{2,0,1:T(2,128)(2,1)S(1)} %get-tuple-element.35), channel_id=1, source_target_pairs={{8,0},{16,8},{24,16},{9,1},{17,9},{25,17},{10,2},{18,10},{26,18},{... | collective-permute-start | bytes 122888 | tf_op jit(solution)/shard_map/ppermute | solution.py:19
  147.0 11.4 %collective-permute-start.2 = (bf16[18,1,320]{2,0,1:T(8,128)(2,1)S(1)}, bf16[18,1,320]{2,0,1:T(8,128)(2,1)S(1)}, u32[]{:S(2)}, u32[]{:S(2)}) collective-permute-start(bf16[18,1,320]{2,0,1:T(8,128)(2,1)S(1)} %get-tuple-element.30), channel_id=1, source_target_pairs={{0,1},{1,2},{2,3},{3,4},{4,5},{5,6},{6,7},{8,9},{9,10},{10,11},{11... | collective-permute-start | bytes 34568 | tf_op jit(solution)/shard_map/ppermute | solution.py:16
  156.3 6.5 %collective-permute-start.3 = (bf16[18,1,320]{2,0,1:T(8,128)(2,1)S(1)}, bf16[18,1,320]{2,0,1:T(8,128)(2,1)S(1)}, u32[]{:S(2)}, u32[]{:S(2)}) collective-permute-start(bf16[18,1,320]{2,0,1:T(8,128)(2,1)S(1)} %get-tuple-element.31), channel_id=1, source_target_pairs={{1,0},{2,1},{3,2},{4,3},{5,4},{6,5},{7,6},{9,8},{10,9},{11,10},{12... | collective-permute-start | bytes 34568 | tf_op jit(solution)/shard_map/ppermute | solution.py:19
  163.6 0.7 copy-start.19
  169.4 39.9 %copy-start.8 = (f32[320]{0:T(512)S(1)}, f32[320]{0:T(512)}, u32[]{:S(2)}) copy-start(f32[320]{0:T(512)} %param.22) | copy-start | bytes 3844
  169.4 39.9 %copy-start.9 = (f32[320]{0:T(512)S(1)}, f32[320]{0:T(512)}, u32[]{:S(2)}) copy-start(f32[320]{0:T(512)} %param.21) | copy-start | bytes 3844
  210.0 5.4 %collective-permute-start.4 = (bf16[1,64,320]{2,0,1:T(2,128)(2,1)S(1)}, bf16[1,64,320]{2,0,1:T(2,128)(2,1)S(1)}, u32[]{:S(2)}, u32[]{:S(2)}) collective-permute-start(bf16[1,64,320]{2,0,1:T(2,128)(2,1)S(1)} %get-tuple-element.32), channel_id=1, source_target_pairs={{0,8},{8,16},{16,24},{1,9},{9,17},{17,25},{2,10},{10,18},{18,26},{... | collective-permute-start | bytes 122888 | tf_op jit(solution)/shard_map/ppermute | solution.py:16
  213.1 6.3 %collective-permute-start.5 = (bf16[1,64,320]{2,0,1:T(2,128)(2,1)S(1)}, bf16[1,64,320]{2,0,1:T(2,128)(2,1)S(1)}, u32[]{:S(2)}, u32[]{:S(2)}) collective-permute-start(bf16[1,64,320]{2,0,1:T(2,128)(2,1)S(1)} %get-tuple-element.33), channel_id=1, source_target_pairs={{8,0},{16,8},{24,16},{9,1},{17,9},{25,17},{10,2},{18,10},{26,18},{... | collective-permute-start | bytes 122888 | tf_op jit(solution)/shard_map/ppermute | solution.py:19
  219.4 24.9 %collective-permute-start.6 = (bf16[18,1,320]{2,0,1:T(8,128)(2,1)S(1)}, bf16[18,1,320]{2,0,1:T(8,128)(2,1)S(1)}, u32[]{:S(2)}, u32[]{:S(2)}) collective-permute-start(bf16[18,1,320]{2,0,1:T(8,128)(2,1)S(1)} %get-tuple-element.28), channel_id=1, source_target_pairs={{0,1},{1,2},{2,3},{3,4},{4,5},{5,6},{6,7},{8,9},{9,10},{10,11},{11... | collective-permute-start | bytes 34568 | tf_op jit(solution)/shard_map/ppermute | solution.py:16
  225.5 18.7 %collective-permute-start.7 = (bf16[18,1,320]{2,0,1:T(8,128)(2,1)S(1)}, bf16[18,1,320]{2,0,1:T(8,128)(2,1)S(1)}, u32[]{:S(2)}, u32[]{:S(2)}) collective-permute-start(bf16[18,1,320]{2,0,1:T(8,128)(2,1)S(1)} %get-tuple-element.29), channel_id=1, source_target_pairs={{1,0},{2,1},{3,2},{4,3},{5,4},{6,5},{7,6},{9,8},{10,9},{11,10},{12... | collective-permute-start | bytes 34568 | tf_op jit(solution)/shard_map/ppermute | solution.py:19
  245.0 1.6 copy-start.16
  250.5 0.7 copy-start.10
  257.2 2.0 copy-start.3
  257.3 1.9 copy-start.17
  259.2 5.7 %copy-start.1 = (bf16[3,3,320,320]{3,2,1,0:T(8,128)(2,1)S(1)}, bf16[3,3,320,320]{3,2,1,0:T(8,128)(2,1)}, u32[]{:S(2)}) copy-start(bf16[3,3,320,320]{3,2,1,0:T(8,128)(2,1)} %param.20) | copy-start | bytes 5529604
Sparse Core Ops, SparseCore 0:
  18.1 30.1 all-gather.2
  138.0 32.4 all-gather.4
where the time goes:
time: 273 us; the launch traced here: 272 us
  blocking collectives  91.3 us (33%)
  local copies, waits for them, and re-layouts  45.5 us (17%)
  waiting for transfers between devices  45.2 us (17%)
  starting transfers between devices  41.2 us (15%)
  matrix products  18.1 us (7%)
  other arithmetic  15.6 us (6%)
  between operations  14.7 us (5%)
    psum x1, blocking collectives, body(): sums, squares = lax.psum((sums, squares), ('rows', 'cols'))  42 us
    psum x1, blocking collectives, body(): sums_two, squares_two = lax.psum((sums_two, squares_two), ('rows', 'cols'))  37.3 us
    ppermute x6, starting transfers between devices, extended(): lax.ppermute(lax.slice_in_dim(block, block.shape[dim] - width, None, axis...  27.5 us
    all_gather x1, waiting for transfers between devices, body(): whole = lax.all_gather(edged_tile, 'cols', axis=1, tiled=True)  27.1 us
    ppermute x6, waiting for transfers between devices, extended(): lax.ppermute(lax.slice_in_dim(block, 0, width, axis=dim), axis, backward)  18 us
    unnamed x52, local copies, waits for them, and re-layouts  16.6 us
    ppermute x6, starting transfers between devices, extended(): lax.ppermute(lax.slice_in_dim(block, 0, width, axis=dim), axis, backward)  13.7 us
    conv_general_dilated x3, matrix products, conv_valid(): lax.conv_general_dilated(padded[None], kernel, (1, 1), 'VALID', dimension...  12.5 us
  transfers between devices with their start and end apart: 14, of which 8 were waited for; matrix products, arithmetic and copies ran while one was open for 14% of the time, Pallas kernels for 0%

commit v1 on v0

--- a/solution.py
+++ b/solution.py
@@ -94,7 +94,7 @@
     padded = extended(act1, (("rows", 0), ("cols", 1)), 1)
     hid1 = conv_valid(padded, conv1a_w)
     sums_two, squares_two = moments(hid1, width_one)
-    sums_two, squares_two = lax.psum((sums_two, squares_two), ("rows", "cols"))
+    sums_two, squares_two = lax.psum(lax.psum((sums_two, squares_two), "cols"), "rows")
     act2 = normalize(hid1, sums_two, squares_two, count_one, norm1b_g, norm1b_b)
     padded_two = extended(act2, (("rows", 0), ("cols", 1)), 1)
     out1 = (latent1.astype(jnp.float32) + conv_valid(padded_two, conv1b_w) + conv1b_b).astype(

time: 273 us -> 213 us (0.78)
  waiting for transfers between devices: 45.2 us -> 7.74 us
  blocking collectives: 91.3 us -> 70 us
  local copies, waits for them, and re-layouts: 45.5 us -> 39.5 us
  starting transfers between devices: 41.2 us -> 44.8 us
    all_gather x1, waiting for transfers between devices: 27.1 us -> 0.01 us  [body(): whole = lax.all_gather(edged_tile, 'cols', axis=1, tiled=True)]
    psum x2, blocking collectives: 43.3 us -> 18.5 us  [the longest x1 12.7 us: body(): lax.psum((sums_two, squares_two), 'cols')]
    ppermute x6, waiting for transfers between devices: 18 us -> 0.13 us  [extended(): lax.ppermute(lax.slice_in_dim(block, 0, width, axis=dim), axis, backward)]
    ppermute x6, starting transfers between devices: 13.7 us -> 24.6 us  [extended(): lax.ppermute(lax.slice_in_dim(block, 0, width, axis=dim), axis, backward)]
    ppermute x6, waiting for transfers between devices: 0.13 us -> 7.57 us  [extended(): lax.ppermute(lax.slice_in_dim(block, block.shape[dim] - width, None, axis...]
    ppermute x6, starting transfers between devices: 27.5 us -> 20.2 us  [extended(): lax.ppermute(lax.slice_in_dim(block, block.shape[dim] - width, None, axis...]
    unnamed x52, local copies, waits for them, and re-layouts: 16.6 us -> 13.7 us
  transfers between devices with their start and end apart: 14 -> 14, of which waited for: 8 -> 7; matrix products, arithmetic and copies ran while one was open for 14% -> 18% of each run, Pallas kernels for 0% -> 0%
where the time goes in v1:
time: 213 us; the launch traced here: 210 us
  blocking collectives  70 us (33%)
  starting transfers between devices  44.8 us (21%)
  local copies, waits for them, and re-layouts  39.5 us (19%)
  matrix products  18.1 us (8%)
  other arithmetic  15 us (7%)
  between operations  14.7 us (7%)
  waiting for transfers between devices  7.74 us (4%)
    psum x1, blocking collectives, body(): sums, squares = lax.psum((sums, squares), ('rows', 'cols'))  43.3 us
    ppermute x6, starting transfers between devices, extended(): lax.ppermute(lax.slice_in_dim(block, 0, width, axis=dim), axis, backward)  24.6 us
    ppermute x6, starting transfers between devices, extended(): lax.ppermute(lax.slice_in_dim(block, block.shape[dim] - width, None, axis...  20.2 us
    unnamed x52, local copies, waits for them, and re-layouts  13.7 us
    psum x1, blocking collectives, body(): lax.psum((sums_two, squares_two), 'cols')  12.7 us
    conv_general_dilated x3, matrix products, conv_valid(): lax.conv_general_dilated(padded[None], kernel, (1, 1), 'VALID', dimension...  12.5 us
    reshape x1, local copies, waits for them, and re-layouts, folder(): weights = kernel.reshape(9 * count, kernel.shape[3])  9.37 us
    conv_general_dilated x11, local copies, waits for them, and re-layouts, conv_valid(): lax.conv_general_dilated(padded[None], kernel, (1, 1), 'VALID', dimension...  8.87 us
  transfers between devices with their start and end apart: 14, of which 7 were waited for; matrix products, arithmetic and copies ran while one was open for 18% of the time, Pallas kernels for 0%

profile of v1, /device:TPU:3, one launch (start us, length us, event | category | flops | bytes accessed | tf_op | source)
XLA Modules:
  0.0 209.9 jit_solution(1590151642484781470)
XLA Ops:
  7.2 1.2 add_convert_fusion
  8.4 1.9 collective-permute-start.9
  10.4 4.3 %collective-permute-start.8 = (bf16[1,16,1280]{2,1,0:T(8,128)(2,1)S(1)}, bf16[1,16,1280]{2,1,0:T(8,128)(2,1)S(1)}, u32[]{:S(2)}, u32[]{:S(2)}) collective-permute-start(bf16[1,16,1280]{2,1,0:T(8,128)(2,1)S(1)} %get-tuple-element.40), channel_id=1, source_target_pairs={{0,8},{8,16},{16,24},{1,9},{9,17},{17,25},{2,10},{10,18},{18,26},{... | collective-permute-start | bytes 122888 | tf_op jit(solution)/shard_map/ppermute | solution.py:16
  14.7 1.1 collective-permute-done.8
  15.7 0.7 pad_maximum_fusion
  16.5 1.6 convert_reduce_fusion.1
  18.6 43.3 %all-reduce.2 = (f32[32]{0:T(128)S(1)}, f32[32]{0:T(128)S(1)}) all-reduce(f32[32]{0:T(128)S(1)} %reduce_sum.100, f32[32]{0:T(128)S(1)} %reduce_sum.97), channel_id=1, replica_groups=mesh['rows'=4,'cols'=8] {'rows','cols'}, use_global_device_ids=true, to_apply=%region_5.6 | all-reduce | flops 64 | bytes 512 | tf_op jit(solution)/shard_map/psum | solution.py:92
  62.3 1.9 fusion.20
  64.3 1.9 collective-permute-start.1
  66.3 4.3 %collective-permute-start = (bf16[1,64,320]{2,0,1:T(2,128)(2,1)S(1)}, bf16[1,64,320]{2,0,1:T(2,128)(2,1)S(1)}, u32[]{:S(2)}, u32[]{:S(2)}) collective-permute-start(bf16[1,64,320]{2,0,1:T(2,128)(2,1)S(1)} %get-tuple-element.36), channel_id=1, source_target_pairs={{0,8},{8,16},{16,24},{1,9},{9,17},{17,25},{2,10},{10,18},{18,26},{... | collective-permute-start | bytes 122888 | tf_op jit(solution)/shard_map/ppermute | solution.py:16
  70.6 1.6 collective-permute-done
  72.2 4.1 %collective-permute-start.3 = (bf16[18,1,320]{2,0,1:T(8,128)(2,1)S(1)}, bf16[18,1,320]{2,0,1:T(8,128)(2,1)S(1)}, u32[]{:S(2)}, u32[]{:S(2)}) collective-permute-start(bf16[18,1,320]{2,0,1:T(8,128)(2,1)S(1)} %get-tuple-element.33), channel_id=1, source_target_pairs={{1,0},{2,1},{3,2},{4,3},{5,4},{6,5},{7,6},{9,8},{10,9},{11,10},{12... | collective-permute-start | bytes 34568 | tf_op jit(solution)/shard_map/ppermute | solution.py:19
  76.3 3.3 %collective-permute-start.2 = (bf16[18,1,320]{2,0,1:T(8,128)(2,1)S(1)}, bf16[18,1,320]{2,0,1:T(8,128)(2,1)S(1)}, u32[]{:S(2)}, u32[]{:S(2)}) collective-permute-start(bf16[18,1,320]{2,0,1:T(8,128)(2,1)S(1)} %get-tuple-element.32), channel_id=1, source_target_pairs={{0,1},{1,2},{2,3},{3,4},{4,5},{5,6},{6,7},{8,9},{9,10},{10,11},{11... | collective-permute-start | bytes 34568 | tf_op jit(solution)/shard_map/ppermute | solution.py:16
  79.6 0.8 collective-permute-done.2
  80.4 0.7 maximum_bitcast_fusion
  81.9 5.1 %select_reduce_fusion.1 = (f32[320]{0:T(512)S(1)}, f32[320]{0:T(512)S(1)}, f32[16,8,9,320]{3,1,2,0:T(8,128)}) fusion(pred[8,9]{0,1:T(8,128)(4,1)S(1)} %copy-done.19, bf16[3,3,320,320]{3,2,1,0:T(8,128)(2,1)S(1)} %copy-done, bf16[18,1,7,2,320]{4,2,3,0,1:T(8,128)(2,1)S(1)} %slice.100, bf16[18,1,8,9,320]{4,2,3,0,1:T(8,128)(2,1)S(1)} %copy.97), kind=kOutput, calls=%fused_computation.22 | convolution fusion | flops 2128619008 | bytes 4311112 | tf_op jit(solution)/shard_map/conv_general_dilated | solution.py:25
  87.4 12.7 %all-reduce.3 = (f32[32]{0:T(128)S(1)}, f32[32]{0:T(128)S(1)}) all-reduce(f32[32]{0:T(128)S(1)} %reduce_sum.112, f32[32]{0:T(128)S(1)} %reduce_sum.106), channel_id=1, replica_groups=mesh['rows'=4,'cols'=8] {'cols'}, use_global_device_ids=true, to_apply=%region_12.13 | all-reduce | flops 64 | bytes 512 | tf_op jit(solution)/shard_map/psum | solution.py:97
  100.2 1.3 slice-done
  101.5 0.8 copy.113
  103.1 8.2 %all-reduce.5 = (f32[32]{0:T(128)S(1)}, f32[32]{0:T(128)S(1)}) all-reduce(f32[32]{0:T(128)S(1)} %reduce_sum.145, f32[32]{0:T(128)S(1)} %reduce_sum.115), channel_id=1, replica_groups=mesh['rows'=4,'cols'=8] {'rows'}, use_global_device_ids=true, to_apply=%region_19.20 | all-reduce | flops 64 | bytes 512 | tf_op jit(solution)/shard_map/psum | solution.py:53
  111.7 3.0 %fusion.11 = bf16[6,128,1280]{2,1,0:T(8,128)(2,1)S(1)} fusion(bf16[6,128,1280]{2,1,0:T(8,128)(2,1)} %all-gather.3.cloned.1.call-done, f32[1280]{0:T(1024)S(1)} %copy-done.6, f32[1280]{0:T(1024)S(1)} %copy-done.7, f32[1280]{0:T(1024)S(1)} %mul.156, f32[1280]{0:T(1024)S(1)} %sub.79, pred[6]{0:T(512)(128)(4,1)S(1)} %compare_and_fusion), kind=kLoop, calls=%fused_computation.20 | loop fusion | flops 10813440 | bytes 3952646 | tf_op jit(solution)/shard_map/jit(_where)/select_n | solution.py:117
  115.3 2.4 %reshape.81 = bf16[6,1,8,17,1280]{4,3,2,0,1:T(8,128)(2,1)} reshape(bf16[6,1,136,1280]{3,2,0,1:T(8,128)(2,1)S(1)} %pad.13) | data formatting | bytes 4177920 | tf_op jit(solution)/shard_map/conv_general_dilated | solution.py:25
  117.7 2.4 %copy.104 = bf16[6,1,8,17,1280]{4,2,3,0,1:T(8,128)(2,1)S(1)} copy(bf16[6,1,8,17,1280]{4,3,2,0,1:T(8,128)(2,1)} %reshape.81) | data formatting | bytes 4177920 | tf_op jit(solution)/shard_map/conv_general_dilated | solution.py:25
  120.2 0.5 copy-done.15
  120.7 3.5 %select_reduce_fusion.3 = (f32[160]{0:T(256)S(1)}, f32[160]{0:T(256)S(1)}, f32[4,8,17,160]{3,1,2,0:T(8,128)S(1)}) fusion(pred[8,17]{0,1:T(8,128)(4,1)S(1)} %copy-done.18, bf16[3,3,1280,160]{2,3,1,0:T(8,128)(2,1)S(1)} %copy-done.15, bf16[6,1,7,2,1280]{4,2,3,0,1:T(8,128)(2,1)S(1)} %slice.109, bf16[6,1,8,17,1280]{4,2,3,0,1:T(8,128)(2,1)S(1)} %copy.104), kind=kOutput, calls=%fused_computation.73 | convolution fusion | flops 2012927744 | bytes 6339976 | tf_op jit(solution)/shard_map/conv_general_dilated | solution.py:25
  125.1 5.8 %all-reduce.4 = (f32[32]{0:T(128)S(1)}, f32[32]{0:T(128)S(1)}, f32[4]{0:T(128)S(1)}, f32[4]{0:T(128)S(1)}) all-reduce(f32[32]{0:T(128)S(1)} %get-tuple-element.22, f32[32]{0:T(128)S(1)} %get-tuple-element.23, f32[4]{0:T(128)S(1)} %reduce_sum.151, f32[4]{0:T(128)S(1)} %reduce_sum.148), channel_id=1, replica_groups=mesh['rows'=4,'cols'=8] {'rows'}, use_global_device_ids=true, to_apply=%region_13.14 | all-reduce | flops 72 | bytes 576 | tf_op jit(solution)/shard_map/psum | solution.py:97
  131.5 4.0 %collective-permute-start.11 = (bf16[1,128,160]{1,2,0:T(8,128)(2,1)S(1)}, bf16[1,128,160]{1,2,0:T(8,128)(2,1)S(1)}, u32[]{:S(2)}, u32[]{:S(2)}) collective-permute-start(bf16[1,128,160]{1,2,0:T(8,128)(2,1)S(1)} %get-tuple-element.39), channel_id=1, source_target_pairs={{8,0},{16,8},{24,16},{9,1},{17,9},{25,17},{10,2},{18,10},{26,18},{... | collective-permute-start | bytes 122888 | tf_op jit(solution)/shard_map/ppermute | solution.py:19
  135.5 2.2 %collective-permute-start.10 = (bf16[1,128,160]{1,2,0:T(8,128)(2,1)S(1)}, bf16[1,128,160]{1,2,0:T(8,128)(2,1)S(1)}, u32[]{:S(2)}, u32[]{:S(2)}) collective-permute-start(bf16[1,128,160]{1,2,0:T(8,128)(2,1)S(1)} %get-tuple-element.38), channel_id=1, source_target_pairs={{0,8},{8,16},{16,24},{1,9},{9,17},{17,25},{2,10},{10,18},{18,26},{... | collective-permute-start | bytes 122888 | tf_op jit(solution)/shard_map/ppermute | solution.py:16
  137.7 2.5 %collective-permute-done.10 = bf16[1,128,160]{1,2,0:T(8,128)(2,1)S(1)} collective-permute-done((bf16[1,128,160]{1,2,0:T(8,128)(2,1)S(1)}, bf16[1,128,160]{1,2,0:T(8,128)(2,1)S(1)}, u32[]{:S(2)}, u32[]{:S(2)}) %collective-permute-start.10) | collective-permute-done | bytes 40992 | tf_op jit(solution)/shard_map/ppermute | solution.py:16
  140.2 0.7 pad_maximum_fusion.1
  141.0 3.0 %copy.98 = f32[16,8,9,320]{3,0,2,1:T(8,128)} copy(f32[16,8,9,320]{3,1,2,0:T(8,128)} %get-tuple-element.50) | data formatting | bytes 2949120 | tf_op jit(solution)/shard_map/conv_general_dilated | solution.py:25
  144.4 2.1 multiply_convert_fusion.1
  146.7 1.9 collective-permute-start.5
  148.6 4.3 %collective-permute-start.4 = (bf16[1,64,320]{2,0,1:T(2,128)(2,1)S(1)}, bf16[1,64,320]{2,0,1:T(2,128)(2,1)S(1)}, u32[]{:S(2)}, u32[]{:S(2)}) collective-permute-start(bf16[1,64,320]{2,0,1:T(2,128)(2,1)S(1)} %get-tuple-element.34), channel_id=1, source_target_pairs={{0,8},{8,16},{16,24},{1,9},{9,17},{17,25},{2,10},{10,18},{18,26},{... | collective-permute-start | bytes 122888 | tf_op jit(solution)/shard_map/ppermute | solution.py:16
  152.9 1.6 collective-permute-done.4
  154.5 10.7 %collective-permute-start.7 = (bf16[18,1,320]{2,0,1:T(8,128)(2,1)S(1)}, bf16[18,1,320]{2,0,1:T(8,128)(2,1)S(1)}, u32[]{:S(2)}, u32[]{:S(2)}) collective-permute-start(bf16[18,1,320]{2,0,1:T(8,128)(2,1)S(1)} %get-tuple-element.31), channel_id=1, source_target_pairs={{1,0},{2,1},{3,2},{4,3},{5,4},{6,5},{7,6},{9,8},{10,9},{11,10},{12... | collective-permute-start | bytes 34568 | tf_op jit(solution)/shard_map/ppermute | solution.py:19
  165.3 1.9 collective-permute-start.6
  167.2 5.4 %copy.111 = bf16[3,3,1280,160]{2,1,0,3:T(4,128)(2,1)} copy(bf16[3,3,1280,160]{2,3,1,0:T(8,128)(2,1)S(1)} %copy-done.4) | data formatting | bytes 7372800 | tf_op args[15]
  172.6 9.4 %reshape.109 = bf16[11520,160,1]{0,1,2:T(8,128)(2,1)} reshape(bf16[3,3,1280,160]{2,1,0,3:T(4,128)(2,1)} %copy.111) | data formatting | bytes 7372800 | tf_op jit(solution)/shard_map/reshape | solution.py:63
  181.9 0.7 maximum_bitcast_fusion.1
  183.1 1.2 copy-done.16
  184.3 3.8 %convolution_select_fusion = f32[16,8,9,320]{3,1,2,0:T(8,128)S(1)} fusion(bf16[3,3,320,320]{3,2,1,0:T(8,128)(2,1)S(1)} %copy-done.16, bf16[18,1,7,2,320]{4,2,3,0,1:T(8,128)(2,1)S(1)} %slice.104, bf16[18,1,8,9,320]{4,2,3,0,1:T(8,128)(2,1)S(1)} %copy.100, pred[8,9]{0,1:T(8,128)(4,1)S(1)} %copy-done.19), kind=kOutput, calls=%fused_computation.42 | convolution fusion | flops 2126776320 | bytes 4308552 | tf_op jit(solution)/shard_map/conv_general_dilated | solution.py:25
  188.5 0.8 copy-done.2
  189.3 0.6 fusion.23
  189.9 1.1 copy.112
  190.9 2.7 %copy.107 = bf16[6,128,1280]{2,1,0:T(8,128)(2,1)S(1)} copy(bf16[6,128,1280]{1,2,0:T(8,128)(2,1)} %all-gather.5.cloned.1.call-done) | data formatting | bytes 3932160 | tf_op jit(solution)/shard_map/all_gather | solution.py:123
  195.8 1.6 copy-done.5
  197.4 5.7 %fusion.45 = bf16[4,128,160]{1,2,0:T(8,128)(2,1)} fusion(bf16[4,128,11520]{2,1,0:T(8,128)(2,1)S(1)} %slice_dynamic-update-slice_fusion.3, bf16[11520,160,1]{0,1,2:T(8,128)(2,1)S(1)} %copy-done.5, f32[160]{0:T(256)S(1)} %copy-done.17, bf16[4,128,1280]{1,2,0:T(8,128)(2,1)} %copy-done.3, s32[]{:T(128)S(6)} %select_n.7), kind=kOutput, calls=%fused_computation.69 | convolution fusion | flops 1887764480 | bytes 15811204 | tf_op jit(solution)/shard_map/dot_general | solution.py:64
  (117 shorter events, 9.0 us)
Async XLA Ops:
  7.2 74.4 %copy-start = (bf16[3,3,320,320]{3,2,1,0:T(8,128)(2,1)S(1)}, bf16[3,3,320,320]{3,2,1,0:T(8,128)(2,1)}, u32[]{:S(2)}) copy-start(bf16[3,3,320,320]{3,2,1,0:T(8,128)(2,1)} %param.20) | copy-start | bytes 5529604
  7.2 55.1 %copy-start.8 = (f32[320]{0:T(512)S(1)}, f32[320]{0:T(512)}, u32[]{:S(2)}) copy-start(f32[320]{0:T(512)} %param.19) | copy-start | bytes 3844
  7.2 55.1 %copy-start.9 = (f32[320]{0:T(512)S(1)}, f32[320]{0:T(512)}, u32[]{:S(2)}) copy-start(f32[320]{0:T(512)} %param.18) | copy-start | bytes 3844
  7.2 93.0 %all-gather.3.cloned.1.call-start = ((), (), s32[]{:S(2)}) async-start(), calls=%async_computation | async-start | bytes 2211840 | tf_op jit(solution)/shard_map/all_gather | solution.py:111
  8.4 6.2 %collective-permute-start.9 = (bf16[1,16,1280]{2,1,0:T(8,128)(2,1)S(1)}, bf16[1,16,1280]{2,1,0:T(8,128)(2,1)S(1)}, u32[]{:S(2)}, u32[]{:S(2)}) collective-permute-start(bf16[1,16,1280]{2,1,0:T(8,128)(2,1)S(1)} %get-tuple-element.41), channel_id=1, source_target_pairs={{8,0},{16,8},{24,16},{9,1},{17,9},{25,17},{10,2},{18,10},{26,18},{... | collective-permute-start | bytes 122888 | tf_op jit(solution)/shard_map/ppermute | solution.py:19
  10.4 5.3 %collective-permute-start.8 = (bf16[1,16,1280]{2,1,0:T(8,128)(2,1)S(1)}, bf16[1,16,1280]{2,1,0:T(8,128)(2,1)S(1)}, u32[]{:S(2)}, u32[]{:S(2)}) collective-permute-start(bf16[1,16,1280]{2,1,0:T(8,128)(2,1)S(1)} %get-tuple-element.40), channel_id=1, source_target_pairs={{0,8},{8,16},{16,24},{1,9},{9,17},{17,25},{2,10},{10,18},{18,26},{... | collective-permute-start | bytes 122888 | tf_op jit(solution)/shard_map/ppermute | solution.py:16
  16.5 174.5 %all-gather.5.cloned.1.call-start = ((), (), s32[]{:S(2)}) async-start(), calls=%async_computation.1 | async-start | bytes 2211840 | tf_op jit(solution)/shard_map/all_gather | solution.py:123
  64.3 6.3 %collective-permute-start.1 = (bf16[1,64,320]{2,0,1:T(2,128)(2,1)S(1)}, bf16[1,64,320]{2,0,1:T(2,128)(2,1)S(1)}, u32[]{:S(2)}, u32[]{:S(2)}) collective-permute-start(bf16[1,64,320]{2,0,1:T(2,128)(2,1)S(1)} %get-tuple-element.37), channel_id=1, source_target_pairs={{8,0},{16,8},{24,16},{9,1},{17,9},{25,17},{10,2},{18,10},{26,18},{... | collective-permute-start | bytes 122888 | tf_op jit(solution)/shard_map/ppermute | solution.py:19
  66.3 5.9 %collective-permute-start = (bf16[1,64,320]{2,0,1:T(2,128)(2,1)S(1)}, bf16[1,64,320]{2,0,1:T(2,128)(2,1)S(1)}, u32[]{:S(2)}, u32[]{:S(2)}) collective-permute-start(bf16[1,64,320]{2,0,1:T(2,128)(2,1)S(1)} %get-tuple-element.36), channel_id=1, source_target_pairs={{0,8},{8,16},{16,24},{1,9},{9,17},{17,25},{2,10},{10,18},{18,26},{... | collective-permute-start | bytes 122888 | tf_op jit(solution)/shard_map/ppermute | solution.py:16
  72.2 7.4 %collective-permute-start.3 = (bf16[18,1,320]{2,0,1:T(8,128)(2,1)S(1)}, bf16[18,1,320]{2,0,1:T(8,128)(2,1)S(1)}, u32[]{:S(2)}, u32[]{:S(2)}) collective-permute-start(bf16[18,1,320]{2,0,1:T(8,128)(2,1)S(1)} %get-tuple-element.33), channel_id=1, source_target_pairs={{1,0},{2,1},{3,2},{4,3},{5,4},{6,5},{7,6},{9,8},{10,9},{11,10},{12... | collective-permute-start | bytes 34568 | tf_op jit(solution)/shard_map/ppermute | solution.py:19
  76.3 4.2 %collective-permute-start.2 = (bf16[18,1,320]{2,0,1:T(8,128)(2,1)S(1)}, bf16[18,1,320]{2,0,1:T(8,128)(2,1)S(1)}, u32[]{:S(2)}, u32[]{:S(2)}) collective-permute-start(bf16[18,1,320]{2,0,1:T(8,128)(2,1)S(1)} %get-tuple-element.32), channel_id=1, source_target_pairs={{0,1},{1,2},{2,3},{3,4},{4,5},{5,6},{6,7},{8,9},{9,10},{10,11},{11... | collective-permute-start | bytes 34568 | tf_op jit(solution)/shard_map/ppermute | solution.py:16
  81.2 0.7 copy-start.19
  100.2 1.3 slice-start
  101.5 10.2 %copy-start.6 = (f32[1280]{0:T(1024)S(1)}, f32[1280]{0:T(1024)}, u32[]{:S(2)}) copy-start(f32[1280]{0:T(1024)} %param.28) | copy-start | bytes 15364
  101.5 10.2 %copy-start.7 = (f32[1280]{0:T(1024)S(1)}, f32[1280]{0:T(1024)}, u32[]{:S(2)}) copy-start(f32[1280]{0:T(1024)} %param.27) | copy-start | bytes 15364
  102.3 9.3 %copy-start.3 = (bf16[4,128,1280]{1,2,0:T(8,128)(2,1)}, bf16[4,128,1280]{1,2,0:T(8,128)(2,1)S(1)}, u32[]{:S(2)}) copy-start(bf16[4,128,1280]{1,2,0:T(8,128)(2,1)S(1)} %copy.113) | copy-start | bytes 3932164
  117.7 2.9 %copy-start.15 = (bf16[3,3,1280,160]{2,3,1,0:T(8,128)(2,1)S(1)}, bf16[3,3,1280,160]{2,3,1,0:T(8,128)(2,1)}, u32[]{:S(2)}) copy-start(bf16[3,3,1280,160]{2,3,1,0:T(8,128)(2,1)} %param.29) | copy-start | bytes 11059204
  117.7 2.9 %copy-start.18 = (pred[8,17]{0,1:T(8,128)(4,1)S(1)}, pred[8,17]{0,1:T(8,128)(4,1)}, u32[]{:S(2)}) copy-start(pred[8,17]{0,1:T(8,128)(4,1)} %constant.75) | copy-start | bytes 412
  124.2 7.1 %copy-start.13 = (f32[160]{0:T(256)S(1)}, f32[160]{0:T(256)}, u32[]{:S(2)}) copy-start(f32[160]{0:T(256)} %param.31) | copy-start | bytes 1924
  124.2 7.0 %copy-start.14 = (f32[160]{0:T(256)S(1)}, f32[160]{0:T(256)}, u32[]{:S(2)}) copy-start(f32[160]{0:T(256)} %param.30) | copy-start | bytes 1924
  131.5 6.2 %collective-permute-start.11 = (bf16[1,128,160]{1,2,0:T(8,128)(2,1)S(1)}, bf16[1,128,160]{1,2,0:T(8,128)(2,1)S(1)}, u32[]{:S(2)}, u32[]{:S(2)}) collective-permute-start(bf16[1,128,160]{1,2,0:T(8,128)(2,1)S(1)} %get-tuple-element.39), channel_id=1, source_target_pairs={{8,0},{16,8},{24,16},{9,1},{17,9},{25,17},{10,2},{18,10},{26,18},{... | collective-permute-start | bytes 122888 | tf_op jit(solution)/shard_map/ppermute | solution.py:19
  135.5 9.0 %copy-start.10 = (f32[320]{0:T(512)S(1)}, f32[320]{0:T(512)}, u32[]{:S(2)}) copy-start(f32[320]{0:T(512)} %param.22) | copy-start | bytes 3844
  135.5 8.9 %copy-start.11 = (f32[320]{0:T(512)S(1)}, f32[320]{0:T(512)}, u32[]{:S(2)}) copy-start(f32[320]{0:T(512)} %param.21) | copy-start | bytes 3844
  135.5 4.7 %collective-permute-start.10 = (bf16[1,128,160]{1,2,0:T(8,128)(2,1)S(1)}, bf16[1,128,160]{1,2,0:T(8,128)(2,1)S(1)}, u32[]{:S(2)}, u32[]{:S(2)}) collective-permute-start(bf16[1,128,160]{1,2,0:T(8,128)(2,1)S(1)} %get-tuple-element.38), channel_id=1, source_target_pairs={{0,8},{8,16},{16,24},{1,9},{9,17},{17,25},{2,10},{10,18},{18,26},{... | collective-permute-start | bytes 122888 | tf_op jit(solution)/shard_map/ppermute | solution.py:16
  144.4 22.8 %copy-start.4 = (bf16[3,3,1280,160]{2,3,1,0:T(8,128)(2,1)S(1)}, bf16[3,3,1280,160]{2,3,1,0:T(8,128)(2,1)}, u32[]{:S(2)}) copy-start(bf16[3,3,1280,160]{2,3,1,0:T(8,128)(2,1)} %param.32) | copy-start | bytes 11059204
  146.7 6.3 %collective-permute-start.5 = (bf16[1,64,320]{2,0,1:T(2,128)(2,1)S(1)}, bf16[1,64,320]{2,0,1:T(2,128)(2,1)S(1)}, u32[]{:S(2)}, u32[]{:S(2)}) collective-permute-start(bf16[1,64,320]{2,0,1:T(2,128)(2,1)S(1)} %get-tuple-element.35), channel_id=1, source_target_pairs={{8,0},{16,8},{24,16},{9,1},{17,9},{25,17},{10,2},{18,10},{26,18},{... | collective-permute-start | bytes 122888 | tf_op jit(solution)/shard_map/ppermute | solution.py:19
  148.6 5.9 %collective-permute-start.4 = (bf16[1,64,320]{2,0,1:T(2,128)(2,1)S(1)}, bf16[1,64,320]{2,0,1:T(2,128)(2,1)S(1)}, u32[]{:S(2)}, u32[]{:S(2)}) collective-permute-start(bf16[1,64,320]{2,0,1:T(2,128)(2,1)S(1)} %get-tuple-element.34), channel_id=1, source_target_pairs={{0,8},{8,16},{16,24},{1,9},{9,17},{17,25},{2,10},{10,18},{18,26},{... | collective-permute-start | bytes 122888 | tf_op jit(solution)/shard_map/ppermute | solution.py:16
  154.5 27.4 %collective-permute-start.7 = (bf16[18,1,320]{2,0,1:T(8,128)(2,1)S(1)}, bf16[18,1,320]{2,0,1:T(8,128)(2,1)S(1)}, u32[]{:S(2)}, u32[]{:S(2)}) collective-permute-start(bf16[18,1,320]{2,0,1:T(8,128)(2,1)S(1)} %get-tuple-element.31), channel_id=1, source_target_pairs={{1,0},{2,1},{3,2},{4,3},{5,4},{6,5},{7,6},{9,8},{10,9},{11,10},{12... | collective-permute-start | bytes 34568 | tf_op jit(solution)/shard_map/ppermute | solution.py:19
  165.3 16.7 %collective-permute-start.6 = (bf16[18,1,320]{2,0,1:T(8,128)(2,1)S(1)}, bf16[18,1,320]{2,0,1:T(8,128)(2,1)S(1)}, u32[]{:S(2)}, u32[]{:S(2)}) collective-permute-start(bf16[18,1,320]{2,0,1:T(8,128)(2,1)S(1)} %get-tuple-element.30), channel_id=1, source_target_pairs={{0,1},{1,2},{2,3},{3,4},{4,5},{5,6},{6,7},{8,9},{9,10},{10,11},{11... | collective-permute-start | bytes 34568 | tf_op jit(solution)/shard_map/ppermute | solution.py:16
  182.7 1.6 copy-start.16
  188.1 1.1 copy-start.2
  188.1 1.1 copy-start.12
  195.3 2.0 copy-start.5
  195.4 1.9 copy-start.17
  197.4 5.7 %copy-start.1 = (bf16[3,3,320,320]{3,2,1,0:T(8,128)(2,1)S(1)}, bf16[3,3,320,320]{3,2,1,0:T(8,128)(2,1)}, u32[]{:S(2)}) copy-start(bf16[3,3,320,320]{3,2,1,0:T(8,128)(2,1)} %param.20) | copy-start | bytes 5529604
Sparse Core Ops, SparseCore 0:
  16.6 32.3 all-gather.2
  141.1 32.8 all-gather.4
